TPU v7x, 128 devices: a whole 4x4x4 slice. The times are simulated.
128 devices in a mesh: outer: 16 (over y_lo, z, core), inner: 8 (over y_hi, x).
Axes of the slice: x: 4, y: 4 (y_hi: 2, y_lo: 2; y = y_hi * 2 + y_lo), z: 4, core: 2. Of those that a mesh axis runs over, the one named last changes fastest.
Arguments:
- sources: float32 [262144, 512], P(('outer', 'inner')), may hold values from -6 to 6
- near_field: float32 [256, 1024, 1024], P(('outer', 'inner')), may hold values from -0.1875 to 0.1875
- project_factor: float32 [262144, 128], P(('outer', 'inner')), may hold values from -0.1875 to 0.1875
- expand_factor: float32 [262144, 128], P(('outer', 'inner')), may hold values from -0.5 to 0.5
- butterfly: float32 [4, 256, 4, 128, 128], P(None, ('outer', 'inner')), may hold values from -0.25 to 0.25
Outputs:
- scattered: float32 [262144, 512], P(('outer', 'inner'))
All inputs are finite; a program needn't handle non-finite values.
Results may differ from a plain program's by a relative error of at most 0.0001.
Values sent between devices are 32-bit elements; how exact they have to be, the bound alone decides.
A program may use at most 256 MiB of HBM per device.

v0:
```python
import jax
import jax.numpy as jnp
from jax import lax
from jax.sharding import PartitionSpec as P

HIGHEST = lax.Precision.HIGHEST


def from_partner(value, axis, bit):
    mask = 2**bit
    pairs = [(source, source ^ mask) for source in range(lax.axis_size(axis))]
    return lax.ppermute(value, axis, pairs)


def swap_section(coeffs, butterfly, section_index, local_bits, inner_bits):
    local_count = coeffs.shape[0]
    low_bit = 2 * section_index
    gathered_set = coeffs[None]
    local_digits = 0
    for position in (low_bit, low_bit + 1):
        if position < local_bits:
            local_digits += 1
            continue
        if position < local_bits + inner_bits:
            partner = from_partner(gathered_set, "inner", position - local_bits)
            my_bit = lax.axis_index("inner") >> position - local_bits & 1
        else:
            partner = from_partner(gathered_set, "outer", position - local_bits - inner_bits)
            my_bit = lax.axis_index("outer") >> position - local_bits - inner_bits & 1
        gathered_set = jnp.where(
            my_bit == 0,
            jnp.concatenate([gathered_set, partner], 0),
            jnp.concatenate([partner, gathered_set], 0),
        )
    flattened = gathered_set.reshape((-1,) + coeffs.shape[1:])
    local_mask = (1 << local_digits) - 1
    digit_mask = local_mask << low_bit
    chosen = []
    for local_node in range(local_count):
        for digit_value in range(4):
            device_part = digit_value >> local_digits
            local_part = local_node & ~digit_mask | (digit_value & local_mask) << low_bit
            chosen.append(flattened[device_part * local_count + local_part])
    inputs = jnp.stack(chosen).reshape(local_count, 4, coeffs.shape[1], coeffs.shape[2])
    return jnp.einsum("likm,limr->lkr", butterfly[section_index], inputs, precision=HIGHEST)


def run_block(source_block, near_field, project_factor, expand_factor, butterfly):
    local_count, leaf_rows, _ = near_field.shape
    rank_width = project_factor.shape[1]
    rhs_count = source_block.shape[1]
    source_rows = source_block.reshape(local_count, leaf_rows, rhs_count)
    coeffs = jnp.einsum(
        "cnk,cnr->ckr",
        project_factor.reshape(local_count, leaf_rows, rank_width),
        source_rows,
        precision=HIGHEST,
    )
    local_bits = local_count.bit_length() - 1
    inner_bits = lax.axis_size("inner").bit_length() - 1
    sections = butterfly.shape[0]
    for section_index in range(sections):
        coeffs = swap_section(coeffs, butterfly, section_index, local_bits, inner_bits)
    near = jnp.einsum("cmn,cnr->cmr", near_field, source_rows, precision=HIGHEST)
    far = jnp.einsum(
        "cnk,ckr->cnr",
        expand_factor.reshape(local_count, leaf_rows, rank_width),
        coeffs,
        precision=HIGHEST,
    )
    return (near + far).reshape(local_count * leaf_rows, rhs_count)


def body(sources, near_field, project_factor, expand_factor, butterfly):
    middle = sources.shape[1] // 2
    first_half = run_block(
        sources[:, :middle], near_field, project_factor, expand_factor, butterfly
    )
    second_half = run_block(
        sources[:, middle:], near_field, project_factor, expand_factor, butterfly
    )
    return jnp.concatenate([first_half, second_half], 1)


def solution(mesh):
    in_specs = (
        P(("outer", "inner"), None),
        P(("outer", "inner"), None, None),
        P(("outer", "inner"), None),
        P(("outer", "inner"), None),
        P(None, ("outer", "inner"), None, None, None),
    )
    out_specs = P(("outer", "inner"), None)
    return jax.shard_map(body, mesh=mesh, in_specs=in_specs, out_specs=out_specs, check_vma=False)
```

profile of v0, /device:TPU:0, one launch (start us, length us, event | category | flops | bytes accessed | tf_op | source)
XLA Modules:
  0.0 125.4 jit_solution(12493311371451587050)
XLA Ops:
  0.0 2.6 %fusion.16 = (f32[2048,256]{1,0:T(8,128)S(1)}, f32[2048,256]{1,0:T(8,128)S(1)}) fusion(f32[2048,512]{1,0:T(8,128)} %param.5), kind=kLoop, calls=%fused_computation.93 | loop fusion | bytes 8388608 | tf_op jit(solution)/shard_map/slice | solution.py:77
  2.7 2.6 %convolution_bitcast_fusion.1 = f32[1,2,128,256]{3,2,1,0:T(8,128)} fusion(f32[2,1024,128]{2,1,0:T(8,128)S(1)} %bitcast.178, f32[2,1024,256]{2,1,0:T(8,128)S(1)} %bitcast.124), kind=kOutput, calls=%fused_computation.4 | convolution fusion | flops 805306368 | bytes 3407872 | tf_op jit(solution)/shard_map/cnk,cnr->ckr/dot_general | solution.py:53
  5.3 1.6 %collective-permute-start = (f32[1,2,128,256]{3,2,1,0:T(8,128)}, f32[1,2,128,256]{3,2,1,0:T(8,128)}, u32[]{:S(2)}, u32[]{:S(2)}) collective-permute-start(f32[1,2,128,256]{3,2,1,0:T(8,128)} %convolution_bitcast_fusion.1), channel_id=1, source_target_pairs={{0,1},{1,0},{2,3},{3,2},{4,5},{5,4},{6,7},{7,6},{8,9},{9,8},{10,11... | collective-permute-start | bytes 786440 | tf_op jit(solution)/shard_map/ppermute | solution.py:12
  6.9 1.9 %convolution_bitcast_fusion = f32[1,2,128,256]{3,2,1,0:T(8,128)S(1)} fusion(f32[2,1024,128]{2,1,0:T(8,128)S(1)} %bitcast.179, f32[2,1024,256]{2,1,0:T(8,128)S(1)} %bitcast.122), kind=kOutput, calls=%fused_computation.3 | convolution fusion | flops 805306368 | bytes 3407872 | tf_op jit(solution)/shard_map/cnk,cnr->ckr/dot_general | solution.py:53
  8.8 0.5 collective-permute-start.7
  9.3 5.5 %collective-permute-done = f32[1,2,128,256]{3,2,1,0:T(8,128)} collective-permute-done((f32[1,2,128,256]{3,2,1,0:T(8,128)}, f32[1,2,128,256]{3,2,1,0:T(8,128)}, u32[]{:S(2)}, u32[]{:S(2)}) %collective-permute-start) | collective-permute-done | bytes 262176 | tf_op jit(solution)/shard_map/ppermute | solution.py:12
  14.8 1.3 %maximum_select_fusion.6 = f32[2,2,128,256]{3,2,1,0:T(8,128)S(1)} fusion(f32[1,2,128,256]{3,2,1,0:T(8,128)} %collective-permute-done, f32[1,2,128,256]{3,2,1,0:T(8,128)} %convolution_bitcast_fusion.1, pred[]{:T(512)S(6)} %eq.34), kind=kLoop, calls=%fused_computation.21 | loop fusion | flops 393216 | bytes 1048577 | tf_op jit(solution)/shard_map/jit(_where)/select_n | solution.py:30
  16.2 1.8 %convolution_bitcast_fusion.9 = f32[1,2,128,256]{2,3,1,0:T(8,128)S(1)} fusion(f32[2,4,128,256]{3,2,1,0:T(8,128)S(1)} %bitcast.177, f32[4,2,4,128,128]{4,3,2,1,0:T(8,128)S(1)} %copy-done.3), kind=kOutput, calls=%fused_computation.12 | convolution fusion | flops 402653184 | bytes 1835008 | tf_op jit(solution)/shard_map/likm,limr->lkr/dot_general | solution.py:45
  18.0 3.2 %collective-permute-start.1 = (f32[1,2,128,256]{2,3,1,0:T(8,128)S(1)}, f32[1,2,128,256]{2,3,1,0:T(8,128)S(1)}, u32[]{:S(2)}, u32[]{:S(2)}) collective-permute-start(f32[1,2,128,256]{2,3,1,0:T(8,128)S(1)} %convolution_bitcast_fusion.9), channel_id=1, source_target_pairs={{0,2},{1,3},{2,0},{3,1},{4,6},{5,7},{6,4},{7,5},{8,10},{9,11},{10,... | collective-permute-start | bytes 786440 | tf_op jit(solution)/shard_map/ppermute | solution.py:12
  21.2 1.1 maximum_select_fusion.10
  22.4 4.7 %collective-permute-done.1 = f32[1,2,128,256]{2,3,1,0:T(8,128)S(1)} collective-permute-done((f32[1,2,128,256]{2,3,1,0:T(8,128)S(1)}, f32[1,2,128,256]{2,3,1,0:T(8,128)S(1)}, u32[]{:S(2)}, u32[]{:S(2)}) %collective-permute-start.1) | collective-permute-done | bytes 262176 | tf_op jit(solution)/shard_map/ppermute | solution.py:12
  27.1 0.8 maximum_select_fusion.7
  27.9 3.2 %collective-permute-start.2 = (f32[2,2,128,256]{2,3,1,0:T(8,128)}, f32[2,2,128,256]{2,3,1,0:T(8,128)}, u32[]{:S(2)}, u32[]{:S(2)}) collective-permute-start(f32[2,2,128,256]{2,3,1,0:T(8,128)} %maximum_select_fusion.7), channel_id=1, source_target_pairs={{0,4},{1,5},{2,6},{3,7},{4,0},{5,1},{6,2},{7,3},{8,12},{9,13},{10,... | collective-permute-start | bytes 1572872 | tf_op jit(solution)/shard_map/ppermute | solution.py:12
  31.1 1.8 %convolution_bitcast_fusion.5 = f32[1,2,128,256]{2,3,1,0:T(8,128)S(1)} fusion(f32[2,4,128,256]{3,2,1,0:T(8,128)S(1)} %bitcast.176, f32[4,2,4,128,128]{4,3,2,1,0:T(8,128)S(1)} %copy-done.3), kind=kOutput, calls=%fused_computation.8 | convolution fusion | flops 402653184 | bytes 1835008 | tf_op jit(solution)/shard_map/likm,limr->lkr/dot_general | solution.py:45
  33.0 2.1 %collective-permute-start.8 = (f32[1,2,128,256]{2,3,1,0:T(8,128)S(1)}, f32[1,2,128,256]{2,3,1,0:T(8,128)}, u32[]{:S(2)}, u32[]{:S(2)}) collective-permute-start(f32[1,2,128,256]{2,3,1,0:T(8,128)S(1)} %convolution_bitcast_fusion.5), channel_id=1, source_target_pairs={{0,2},{1,3},{2,0},{3,1},{4,6},{5,7},{6,4},{7,5},{8,10},{9,11},{10,... | collective-permute-start | bytes 786440 | tf_op jit(solution)/shard_map/ppermute | solution.py:12
  35.1 6.0 %collective-permute-done.8 = f32[1,2,128,256]{2,3,1,0:T(8,128)} collective-permute-done((f32[1,2,128,256]{2,3,1,0:T(8,128)S(1)}, f32[1,2,128,256]{2,3,1,0:T(8,128)}, u32[]{:S(2)}, u32[]{:S(2)}) %collective-permute-start.8) | collective-permute-done | bytes 262176 | tf_op jit(solution)/shard_map/ppermute | solution.py:12
  41.1 1.1 maximum_select_fusion.11
  42.1 0.4 collective-permute-start.9
  42.6 1.8 %maximum_select_fusion = f32[4,2,128,256]{2,3,1,0:T(8,128)S(1)} fusion(f32[2,2,128,256]{2,3,1,0:T(8,128)} %collective-permute-done.2, f32[2,2,128,256]{2,3,1,0:T(8,128)} %maximum_select_fusion.7, pred[]{:T(512)S(6)} %eq.32), kind=kLoop, calls=%fused_computation.14 | loop fusion | flops 786432 | bytes 2097153 | tf_op jit(solution)/shard_map/jit(_where)/select_n | solution.py:30
  44.6 1.1 convolution_bitcast_fusion.8
  45.6 0.3 collective-permute-start.3
  45.9 8.8 %collective-permute-done.9 = f32[2,2,128,256]{2,3,1,0:T(8,128)S(1)} collective-permute-done((f32[2,2,128,256]{2,3,1,0:T(8,128)S(1)}, f32[2,2,128,256]{2,3,1,0:T(8,128)S(1)}, u32[]{:S(2)}, u32[]{:S(2)}) %collective-permute-start.9) | collective-permute-done | bytes 524320 | tf_op jit(solution)/shard_map/ppermute | solution.py:12
  55.0 1.1 convolution_bitcast_fusion.4
  56.2 0.8 maximum_select_fusion.8
  57.0 1.9 %collective-permute-start.4 = (f32[2,2,128,256]{2,3,1,0:T(8,128)}, f32[2,2,128,256]{2,3,1,0:T(8,128)}, u32[]{:S(2)}, u32[]{:S(2)}) collective-permute-start(f32[2,2,128,256]{2,3,1,0:T(8,128)} %maximum_select_fusion.8), channel_id=1, source_target_pairs={{0,16},{8,24},{16,0},{24,8},{32,48},{40,56},{48,32},{56,40},{64,80... | collective-permute-start | bytes 1572872 | tf_op jit(solution)/shard_map/ppermute | solution.py:12
  58.9 10.0 %fusion.17 = f32[2,1024,256]{2,1,0:T(8,128)} fusion(f32[2,1024,1024]{2,1,0:T(8,128)} %param.6, f32[2,1024,256]{2,1,0:T(8,128)S(1)} %bitcast.125), kind=kOutput, calls=%fused_computation.94 | convolution fusion | flops 6442450944 | bytes 12582912 | tf_op jit(solution)/shard_map/cmn,cnr->cmr/dot_general | solution.py:64
  68.9 1.1 maximum_select_fusion.12
  70.2 1.6 %collective-permute-done.4 = f32[2,2,128,256]{2,3,1,0:T(8,128)} collective-permute-done((f32[2,2,128,256]{2,3,1,0:T(8,128)}, f32[2,2,128,256]{2,3,1,0:T(8,128)}, u32[]{:S(2)}, u32[]{:S(2)}) %collective-permute-start.4) | collective-permute-done | bytes 524320 | tf_op jit(solution)/shard_map/ppermute | solution.py:12
  71.8 1.6 %maximum_select_fusion.1 = f32[4,2,128,256]{2,3,1,0:T(8,128)S(1)} fusion(f32[2,2,128,256]{2,3,1,0:T(8,128)} %collective-permute-done.4, f32[2,2,128,256]{2,3,1,0:T(8,128)} %maximum_select_fusion.8, pred[]{:T(512)S(6)} %eq.30), kind=kLoop, calls=%fused_computation.15 | loop fusion | flops 786432 | bytes 2097153 | tf_op jit(solution)/shard_map/jit(_where)/select_n | solution.py:30
  73.6 1.1 convolution_bitcast_fusion.7
  74.7 3.8 %collective-permute-start.5 = (f32[1,2,128,256]{2,3,1,0:T(8,128)S(1)}, f32[1,2,128,256]{2,3,1,0:T(8,128)S(1)}, u32[]{:S(2)}, u32[]{:S(2)}) collective-permute-start(f32[1,2,128,256]{2,3,1,0:T(8,128)S(1)} %convolution_bitcast_fusion.7), channel_id=1, source_target_pairs={{0,32},{8,40},{16,48},{24,56},{32,0},{40,8},{48,16},{56,24},{64,96... | collective-permute-start | bytes 786440 | tf_op jit(solution)/shard_map/ppermute | solution.py:12
  78.4 6.5 %collective-permute-done.11 = f32[2,2,128,256]{2,3,1,0:T(8,128)S(1)} collective-permute-done((f32[2,2,128,256]{2,3,1,0:T(8,128)S(1)}, f32[2,2,128,256]{2,3,1,0:T(8,128)S(1)}, u32[]{:S(2)}, u32[]{:S(2)}) %collective-permute-start.11) | collective-permute-done | bytes 524320 | tf_op jit(solution)/shard_map/ppermute | solution.py:12
  85.1 1.1 convolution_bitcast_fusion.3
  86.2 3.7 %collective-permute-start.12 = (f32[1,2,128,256]{2,3,1,0:T(8,128)S(1)}, f32[1,2,128,256]{2,3,1,0:T(8,128)}, u32[]{:S(2)}, u32[]{:S(2)}) collective-permute-start(f32[1,2,128,256]{2,3,1,0:T(8,128)S(1)} %convolution_bitcast_fusion.3), channel_id=1, source_target_pairs={{0,32},{8,40},{16,48},{24,56},{32,0},{40,8},{48,16},{56,24},{64,96... | collective-permute-start | bytes 786440 | tf_op jit(solution)/shard_map/ppermute | solution.py:12
  89.8 2.6 %collective-permute-done.5 = f32[1,2,128,256]{2,3,1,0:T(8,128)S(1)} collective-permute-done((f32[1,2,128,256]{2,3,1,0:T(8,128)S(1)}, f32[1,2,128,256]{2,3,1,0:T(8,128)S(1)}, u32[]{:S(2)}, u32[]{:S(2)}) %collective-permute-start.5) | collective-permute-done | bytes 262176 | tf_op jit(solution)/shard_map/ppermute | solution.py:12
  92.5 0.8 maximum_select_fusion.9
  93.3 0.4 collective-permute-start.6
  93.7 10.0 %fusion.18 = f32[2,1024,256]{2,1,0:T(8,128)} fusion(f32[2,1024,1024]{2,1,0:T(8,128)} %param.6, f32[2,1024,256]{2,1,0:T(8,128)S(1)} %bitcast.123), kind=kOutput, calls=%fused_computation.95 | convolution fusion | flops 6442450944 | bytes 12582912 | tf_op jit(solution)/shard_map/cmn,cnr->cmr/dot_general | solution.py:64
  103.7 1.1 maximum_select_fusion.13
  104.8 1.7 %collective-permute-start.13 = (f32[2,2,128,256]{2,3,1,0:T(8,128)S(1)}, f32[2,2,128,256]{2,3,1,0:T(8,128)S(1)}, u32[]{:S(2)}, u32[]{:S(2)}) collective-permute-start(f32[2,2,128,256]{2,3,1,0:T(8,128)S(1)} %maximum_select_fusion.13), channel_id=1, source_target_pairs={{0,64},{8,72},{16,80},{24,88},{32,96},{40,104},{48,112},{56,120},{... | collective-permute-start | bytes 1572872 | tf_op jit(solution)/shard_map/ppermute | solution.py:12
  106.5 1.6 %maximum_select_fusion.2 = f32[4,2,128,256]{2,3,1,0:T(8,128)S(1)} fusion(f32[2,2,128,256]{2,3,1,0:T(8,128)} %collective-permute-done.6, f32[2,2,128,256]{2,3,1,0:T(8,128)} %maximum_select_fusion.9, pred[]{:T(512)S(6)} %eq.28), kind=kLoop, calls=%fused_computation.16 | loop fusion | flops 786432 | bytes 2097153 | tf_op jit(solution)/shard_map/jit(_where)/select_n | solution.py:30
  108.3 1.1 convolution_bitcast_fusion.6
  109.4 8.1 %collective-permute-done.13 = f32[2,2,128,256]{2,3,1,0:T(8,128)S(1)} collective-permute-done((f32[2,2,128,256]{2,3,1,0:T(8,128)S(1)}, f32[2,2,128,256]{2,3,1,0:T(8,128)S(1)}, u32[]{:S(2)}, u32[]{:S(2)}) %collective-permute-start.13) | collective-permute-done | bytes 524320 | tf_op jit(solution)/shard_map/ppermute | solution.py:12
  117.7 1.1 convolution_bitcast_fusion.2
  118.8 0.4 copy-done.7
  119.1 1.8 %bitcast_add_fusion.1 = f32[2,1024,256]{2,1,0:T(8,128)S(1)} fusion(f32[2,1024,256]{2,1,0:T(8,128)S(1)} %copy-done.7, f32[2,256,128]{2,1,0:T(8,128)S(1)} %convolution_bitcast_fusion.6, f32[2,1024,128]{2,1,0:T(8,128)S(1)} %bitcast.120), kind=kOutput, calls=%fused_computation.2 | convolution fusion | flops 805830656 | bytes 5505024 | tf_op jit(solution)/shard_map/cnk,ckr->cnr/dot_general | solution.py:65
  121.0 1.8 %bitcast_add_fusion = f32[2,1024,256]{2,1,0:T(8,128)S(1)} fusion(f32[2,1024,256]{2,1,0:T(8,128)S(1)} %copy-done.8, f32[2,256,128]{2,1,0:T(8,128)S(1)} %convolution_bitcast_fusion.2, f32[2,1024,128]{2,1,0:T(8,128)S(1)} %bitcast.121), kind=kOutput, calls=%fused_computation.1 | convolution fusion | flops 805830656 | bytes 5505024 | tf_op jit(solution)/shard_map/cnk,ckr->cnr/dot_general | solution.py:65
  122.8 2.5 %pad_maximum_fusion = f32[2048,512]{1,0:T(8,128)} fusion(f32[2048,256]{1,0:T(8,128)S(1)} %bitcast.127, f32[2048,256]{1,0:T(8,128)S(1)} %bitcast.126), kind=kLoop, calls=%fused_computation | loop fusion | flops 1048576 | bytes 8388608 | tf_op jit(solution)/shard_map/concatenate | solution.py:82
  (80 shorter events, 1.3 us)
Async XLA Ops:
  0.0 118.7 %copy-start = (f32[2048,128]{1,0:T(8,128)S(1)}, f32[2048,128]{1,0:T(8,128)}, u32[]{:S(2)}) copy-start(f32[2048,128]{1,0:T(8,128)} %param.8) | copy-start | bytes 3145732
  0.0 2.7 %copy-start.9 = (f32[2048,128]{1,0:T(8,128)S(1)}, f32[2048,128]{1,0:T(8,128)}, u32[]{:S(2)}) copy-start(f32[2048,128]{1,0:T(8,128)} %param.7) | copy-start | bytes 3145732
  2.6 6.2 %copy-start.1 = (f32[2048,256]{1,0:T(8,128)}, f32[2048,256]{1,0:T(8,128)S(1)}, u32[]{:S(2)}) copy-start(f32[2048,256]{1,0:T(8,128)S(1)} %get-tuple-element.5) | copy-start | bytes 6291460
  5.3 9.5 %collective-permute-start = (f32[1,2,128,256]{3,2,1,0:T(8,128)}, f32[1,2,128,256]{3,2,1,0:T(8,128)}, u32[]{:S(2)}, u32[]{:S(2)}) collective-permute-start(f32[1,2,128,256]{3,2,1,0:T(8,128)} %convolution_bitcast_fusion.1), channel_id=1, source_target_pairs={{0,1},{1,0},{2,3},{3,2},{4,5},{5,4},{6,7},{7,6},{8,9},{9,8},{10,11... | collective-permute-start | bytes 786440 | tf_op jit(solution)/shard_map/ppermute | solution.py:12
  8.8 12.4 %collective-permute-start.7 = (f32[1,2,128,256]{3,2,1,0:T(8,128)S(1)}, f32[1,2,128,256]{3,2,1,0:T(8,128)}, u32[]{:S(2)}, u32[]{:S(2)}) collective-permute-start(f32[1,2,128,256]{3,2,1,0:T(8,128)S(1)} %convolution_bitcast_fusion), channel_id=1, source_target_pairs={{0,1},{1,0},{2,3},{3,2},{4,5},{5,4},{6,7},{7,6},{8,9},{9,8},{10,11... | collective-permute-start | bytes 786440 | tf_op jit(solution)/shard_map/ppermute | solution.py:12
  9.3 6.8 %copy-start.3 = (f32[4,2,4,128,128]{4,3,2,1,0:T(8,128)S(1)}, f32[4,2,4,128,128]{4,3,2,1,0:T(8,128)}, u32[]{:S(2)}) copy-start(f32[4,2,4,128,128]{4,3,2,1,0:T(8,128)} %param.9) | copy-start | bytes 6291460
  18.0 9.1 %collective-permute-start.1 = (f32[1,2,128,256]{2,3,1,0:T(8,128)S(1)}, f32[1,2,128,256]{2,3,1,0:T(8,128)S(1)}, u32[]{:S(2)}, u32[]{:S(2)}) collective-permute-start(f32[1,2,128,256]{2,3,1,0:T(8,128)S(1)} %convolution_bitcast_fusion.9), channel_id=1, source_target_pairs={{0,2},{1,3},{2,0},{3,1},{4,6},{5,7},{6,4},{7,5},{8,10},{9,11},{10,... | collective-permute-start | bytes 786440 | tf_op jit(solution)/shard_map/ppermute | solution.py:12
  27.9 14.6 %collective-permute-start.2 = (f32[2,2,128,256]{2,3,1,0:T(8,128)}, f32[2,2,128,256]{2,3,1,0:T(8,128)}, u32[]{:S(2)}, u32[]{:S(2)}) collective-permute-start(f32[2,2,128,256]{2,3,1,0:T(8,128)} %maximum_select_fusion.7), channel_id=1, source_target_pairs={{0,4},{1,5},{2,6},{3,7},{4,0},{5,1},{6,2},{7,3},{8,12},{9,13},{10,... | collective-permute-start | bytes 1572872 | tf_op jit(solution)/shard_map/ppermute | solution.py:12
  33.0 8.1 %collective-permute-start.8 = (f32[1,2,128,256]{2,3,1,0:T(8,128)S(1)}, f32[1,2,128,256]{2,3,1,0:T(8,128)}, u32[]{:S(2)}, u32[]{:S(2)}) collective-permute-start(f32[1,2,128,256]{2,3,1,0:T(8,128)S(1)} %convolution_bitcast_fusion.5), channel_id=1, source_target_pairs={{0,2},{1,3},{2,0},{3,1},{4,6},{5,7},{6,4},{7,5},{8,10},{9,11},{10,... | collective-permute-start | bytes 786440 | tf_op jit(solution)/shard_map/ppermute | solution.py:12
  42.1 2.4 %copy-start.4 = (f32[4,2,4,128,128]{4,3,2,1,0:T(8,128)S(1)}, f32[4,2,4,128,128]{4,3,2,1,0:T(8,128)}, u32[]{:S(2)}) copy-start(f32[4,2,4,128,128]{4,3,2,1,0:T(8,128)} %param.9) | copy-start | bytes 6291460
  42.1 12.6 %collective-permute-start.9 = (f32[2,2,128,256]{2,3,1,0:T(8,128)S(1)}, f32[2,2,128,256]{2,3,1,0:T(8,128)S(1)}, u32[]{:S(2)}, u32[]{:S(2)}) collective-permute-start(f32[2,2,128,256]{2,3,1,0:T(8,128)S(1)} %maximum_select_fusion.11), channel_id=1, source_target_pairs={{0,4},{1,5},{2,6},{3,7},{4,0},{5,1},{6,2},{7,3},{8,12},{9,13},{10,... | collective-permute-start | bytes 1572872 | tf_op jit(solution)/shard_map/ppermute | solution.py:12
  45.6 10.5 %collective-permute-start.3 = (f32[1,2,128,256]{2,3,1,0:T(8,128)S(1)}, f32[1,2,128,256]{2,3,1,0:T(8,128)S(1)}, u32[]{:S(2)}, u32[]{:S(2)}) collective-permute-start(f32[1,2,128,256]{2,3,1,0:T(8,128)S(1)} %convolution_bitcast_fusion.8), channel_id=1, source_target_pairs={{0,8},{8,0},{16,24},{24,16},{32,40},{40,32},{48,56},{56,48},{64,72... | collective-permute-start | bytes 786440 | tf_op jit(solution)/shard_map/ppermute | solution.py:12
  54.9 4.0 %copy-start.2 = (f32[2048,256]{1,0:T(8,128)S(1)}, f32[2048,256]{1,0:T(8,128)}, u32[]{:S(2)}) copy-start(f32[2048,256]{1,0:T(8,128)} %copy-done.1) | copy-start | bytes 6291460
  56.0 12.9 %collective-permute-start.10 = (f32[1,2,128,256]{2,3,1,0:T(8,128)S(1)}, f32[1,2,128,256]{2,3,1,0:T(8,128)}, u32[]{:S(2)}, u32[]{:S(2)}) collective-permute-start(f32[1,2,128,256]{2,3,1,0:T(8,128)S(1)} %convolution_bitcast_fusion.4), channel_id=1, source_target_pairs={{0,8},{8,0},{16,24},{24,16},{32,40},{40,32},{48,56},{56,48},{64,72... | collective-permute-start | bytes 786440 | tf_op jit(solution)/shard_map/ppermute | solution.py:12
  57.0 14.8 %collective-permute-start.4 = (f32[2,2,128,256]{2,3,1,0:T(8,128)}, f32[2,2,128,256]{2,3,1,0:T(8,128)}, u32[]{:S(2)}, u32[]{:S(2)}) collective-permute-start(f32[2,2,128,256]{2,3,1,0:T(8,128)} %maximum_select_fusion.8), channel_id=1, source_target_pairs={{0,16},{8,24},{16,0},{24,8},{32,48},{40,56},{48,32},{56,40},{64,80... | collective-permute-start | bytes 1572872 | tf_op jit(solution)/shard_map/ppermute | solution.py:12
  70.0 3.6 %copy-start.5 = (f32[4,2,4,128,128]{4,3,2,1,0:T(8,128)S(1)}, f32[4,2,4,128,128]{4,3,2,1,0:T(8,128)}, u32[]{:S(2)}) copy-start(f32[4,2,4,128,128]{4,3,2,1,0:T(8,128)} %param.9) | copy-start | bytes 6291460
  70.0 14.9 %collective-permute-start.11 = (f32[2,2,128,256]{2,3,1,0:T(8,128)S(1)}, f32[2,2,128,256]{2,3,1,0:T(8,128)S(1)}, u32[]{:S(2)}, u32[]{:S(2)}) collective-permute-start(f32[2,2,128,256]{2,3,1,0:T(8,128)S(1)} %maximum_select_fusion.12), channel_id=1, source_target_pairs={{0,16},{8,24},{16,0},{24,8},{32,48},{40,56},{48,32},{56,40},{64,80... | collective-permute-start | bytes 1572872 | tf_op jit(solution)/shard_map/ppermute | solution.py:12
  74.7 17.8 %collective-permute-start.5 = (f32[1,2,128,256]{2,3,1,0:T(8,128)S(1)}, f32[1,2,128,256]{2,3,1,0:T(8,128)S(1)}, u32[]{:S(2)}, u32[]{:S(2)}) collective-permute-start(f32[1,2,128,256]{2,3,1,0:T(8,128)S(1)} %convolution_bitcast_fusion.7), channel_id=1, source_target_pairs={{0,32},{8,40},{16,48},{24,56},{32,0},{40,8},{48,16},{56,24},{64,96... | collective-permute-start | bytes 786440 | tf_op jit(solution)/shard_map/ppermute | solution.py:12
  86.2 17.5 %collective-permute-start.12 = (f32[1,2,128,256]{2,3,1,0:T(8,128)S(1)}, f32[1,2,128,256]{2,3,1,0:T(8,128)}, u32[]{:S(2)}, u32[]{:S(2)}) collective-permute-start(f32[1,2,128,256]{2,3,1,0:T(8,128)S(1)} %convolution_bitcast_fusion.3), channel_id=1, source_target_pairs={{0,32},{8,40},{16,48},{24,56},{32,0},{40,8},{48,16},{56,24},{64,96... | collective-permute-start | bytes 786440 | tf_op jit(solution)/shard_map/ppermute | solution.py:12
  93.3 13.2 %collective-permute-start.6 = (f32[2,2,128,256]{2,3,1,0:T(8,128)}, f32[2,2,128,256]{2,3,1,0:T(8,128)}, u32[]{:S(2)}, u32[]{:S(2)}) collective-permute-start(f32[2,2,128,256]{2,3,1,0:T(8,128)} %maximum_select_fusion.9), channel_id=1, source_target_pairs={{0,64},{8,72},{16,80},{24,88},{32,96},{40,104},{48,112},{56,120},{... | collective-permute-start | bytes 1572872 | tf_op jit(solution)/shard_map/ppermute | solution.py:12
  104.8 3.5 %copy-start.6 = (f32[4,2,4,128,128]{4,3,2,1,0:T(8,128)S(1)}, f32[4,2,4,128,128]{4,3,2,1,0:T(8,128)}, u32[]{:S(2)}) copy-start(f32[4,2,4,128,128]{4,3,2,1,0:T(8,128)} %param.9) | copy-start | bytes 6291460
  104.8 12.7 %collective-permute-start.13 = (f32[2,2,128,256]{2,3,1,0:T(8,128)S(1)}, f32[2,2,128,256]{2,3,1,0:T(8,128)S(1)}, u32[]{:S(2)}, u32[]{:S(2)}) collective-permute-start(f32[2,2,128,256]{2,3,1,0:T(8,128)S(1)} %maximum_select_fusion.13), channel_id=1, source_target_pairs={{0,64},{8,72},{16,80},{24,88},{32,96},{40,104},{48,112},{56,120},{... | collective-permute-start | bytes 1572872 | tf_op jit(solution)/shard_map/ppermute | solution.py:12
  117.5 1.6 %copy-start.7 = (f32[2,1024,256]{2,1,0:T(8,128)S(1)}, f32[2,1024,256]{2,1,0:T(8,128)}, u32[]{:S(2)}) copy-start(f32[2,1024,256]{2,1,0:T(8,128)} %fusion.17) | copy-start | bytes 6291460
  119.1 1.9 %copy-start.8 = (f32[2,1024,256]{2,1,0:T(8,128)S(1)}, f32[2,1024,256]{2,1,0:T(8,128)}, u32[]{:S(2)}) copy-start(f32[2,1024,256]{2,1,0:T(8,128)} %fusion.18) | copy-start | bytes 6291460
where the time goes:
time: 126 us; the launch traced here: 125 us
  waiting for transfers between devices  43.7 us (35%)
  matrix products  38.3 us (30%)
  starting transfers between devices  23 us (18%)
  other arithmetic  16.1 us (13%)
  local copies, waits for them, and re-layouts  3.6 us (3%)
    ppermute x14, waiting for transfers between devices, from_partner(): return lax.ppermute(value, axis, pairs)  43.7 us
    ppermute x14, starting transfers between devices, from_partner(): return lax.ppermute(value, axis, pairs)  23 us
    dot_general x2, matrix products, run_block(): jnp.einsum('cmn,cnr->cmr', near_field, source_rows, precision=HIGHEST)  20 us
    select_n x14, other arithmetic, swap_section(): jnp.where(my_bit == 0, jnp.concatenate([gathered_set, partner], 0), jnp.c...  13.4 us
    dot_general x8, matrix products, swap_section(): jnp.einsum('likm,limr->lkr', butterfly[section_index], inputs, precision=...  10 us
    dot_general x2, matrix products, run_block(): jnp.einsum('cnk,cnr->ckr', project_factor.reshape(local_count, leaf_rows,...  4.53 us
    dot_general x2, matrix products, run_block(): jnp.einsum('cnk,ckr->cnr', expand_factor.reshape(local_count, leaf_rows,...  3.69 us
    slice x1, local copies, waits for them, and re-layouts, body(): sources[:, :middle]  2.64 us
  transfers between devices with their start and end apart: 14, of which 8 were waited for; matrix products, arithmetic and copies ran while one was open for 35% of the time, Pallas kernels for 0%

commit v1 on v0

v1 whole, which is shorter than its diff:
```python
import functools

import jax
import jax.numpy as jnp
from jax import lax
from jax.experimental import pallas as pl
from jax.experimental.pallas import tpu as pltpu
from jax.sharding import PartitionSpec as P

MESH = pl.DeviceIdType.MESH
LANES = 128
SUBS = 8
TILES = 8
X1, X2, Y2, Z1, CO, FW, Y1, Z2 = range(8)
AT_SEND, AT_L0, AT_L1, AT_SUM1, AT_FWD, AT_L2, AT_L3, AT_SUM3 = 0, 2, 4, 6, 8, 9, 11, 13
NEAR_AT = 0


def halves(value):
    high = value.astype(jnp.bfloat16)
    low = (value - high.astype(jnp.float32)).astype(jnp.bfloat16)
    return high, low


def dot(left, right):
    return jnp.dot(left, right, preferred_element_type=jnp.float32)


def product(stacked, value):
    rows = stacked.shape[0] // 2
    high, low = halves(value)
    both = dot(stacked, jnp.concatenate([high, low], 1))
    return both[:rows, :LANES] + both[:rows, LANES:] + both[rows:, :LANES]


def kernel(
    src, near, proj, expand, fly, out,
    s_v, n_v, p_v, e_v, b_v, s_hi, s_lo, p_t, e_w, l0, l1, l2, l3, w1, w3,
    xb, xr, yb, yr, zo, zs, zr, cb, czr, cor, cfr, db, dr, fo, fs, fr,
    s_sem, n_sem, p_sem, e_sem, b_sem, w_send, w_recv, send_sem, recv_sem,
):
    outer = lax.axis_index("outer")
    inner = lax.axis_index("inner")
    x_lo, x_hi, y_hi = inner % 2, inner // 2 % 2, inner // 4
    core, z_lo, z_hi, y_lo = outer % 2, outer // 2 % 2, outer // 4 % 2, outer // 8
    inner_x1 = inner + 1 - 2 * x_lo
    inner_x2 = inner + 2 - 4 * x_hi
    inner_y2 = inner + 4 - 8 * y_hi
    outer_co = outer + 1 - 2 * core
    outer_z1 = outer + 2 - 4 * z_lo
    outer_z2 = outer + 4 - 8 * z_hi
    outer_y1 = outer + 8 - 16 * y_lo
    where = {
        X1: (outer, inner_x1),
        X2: (outer, inner_x2),
        Y2: (outer, inner_y2),
        Z1: (outer_z1, inner),
        CO: (outer_co, inner),
        FW: (outer_co, inner),
        Y1: (outer_y1, inner),
        Z2: (outer_z2, inner),
    }
    buffers = {
        X1: (xb, xr), X2: (yb, yr), Y2: (zs, zr), Z1: (cb, czr),
        CO: (cb, cor), FW: (czr, cfr), Y1: (db, dr), Z2: (fs, fr),
    }

    def exchange(step, sub):
        source, target = buffers[step]
        return pltpu.make_async_remote_copy(
            src_ref=source.at[sub],
            dst_ref=target.at[sub],
            send_sem=send_sem.at[step, sub],
            recv_sem=recv_sem.at[step, sub],
            device_id=where[step],
            device_id_type=MESH,
        )

    barrier = pltpu.get_barrier_semaphore()
    for step in (X1, X2, Y2, Z1, CO, Y1, Z2):
        pl.semaphore_signal(barrier, inc=1, device_id=where[step], device_id_type=MESH)

    def load_p(node):
        return pltpu.make_async_copy(proj.at[node], p_v.at[node], p_sem.at[node])

    def load_s(panel):
        return pltpu.make_async_copy(
            src.at[:, :, pl.ds(panel * LANES, LANES)], s_v.at[panel], s_sem.at[panel]
        )

    def load_b(level):
        return pltpu.make_async_copy(fly.at[level], b_v.at[level], b_sem.at[level])

    def load_n(tile):
        return pltpu.make_async_copy(near.at[tile], n_v.at[tile], n_sem.at[tile])

    load_e = pltpu.make_async_copy(expand, e_v, e_sem.at[0])

    load_p(0).start()
    load_p(1).start()
    for panel in range(4):
        load_s(panel).start()
    load_b(0).start()

    for node in range(2):
        load_p(node).wait()
        high, low = halves(p_v[node].T)
        p_t[node, 0:LANES, :] = high
        p_t[node, LANES : 2 * LANES, :] = low

    pl.semaphore_wait(barrier, 7)
    send_w1 = pltpu.make_async_remote_copy(
        src_ref=fly.at[1, :, 1 - y_hi],
        dst_ref=w1,
        send_sem=w_send.at[0],
        recv_sem=w_recv.at[0],
        device_id=where[Y2],
        device_id_type=MESH,
    )
    send_w3 = pltpu.make_async_remote_copy(
        src_ref=fly.at[3, :, :, 1 - z_hi],
        dst_ref=w3,
        send_sem=w_send.at[1],
        recv_sem=w_recv.at[1],
        device_id=where[Z2],
        device_id_type=MESH,
    )
    send_w1.start()
    send_w3.start()

    def project(panel, _):
        load_s(panel).wait()
        for node in range(2):
            high, low = halves(s_v[panel, node])
            columns = pl.ds(pl.multiple_of(panel * LANES, LANES), LANES)
            s_hi[node, :, columns] = high
            s_lo[node, :, columns] = low
            both = dot(p_t[node], jnp.concatenate([high, low], 1))
            xb[2 * panel + node] = (
                both[:LANES, :LANES] + both[:LANES, LANES:] + both[LANES:, :LANES]
            )

        @pl.when(panel == 0)
        def _():
            exchange(X1, 0).start()
            exchange(X1, 1).start()
            for level in range(1, 4):
                load_b(level).start()
            load_n(0).start()
            load_n(1).start()

        return 0

    lax.fori_loop(0, 4, project, 0)

    load_b(0).wait()
    for node in range(2):
        for block in range(4):
            high, low = halves(b_v[0, node, (x_lo + block // 2) % 2, block % 2])
            columns = slice(block * LANES, block * LANES + LANES)
            l0[node * LANES : node * LANES + LANES, columns] = high
            l0[(2 + node) * LANES : (3 + node) * LANES, columns] = low

    def prepare_1():
        load_b(1).wait()
        send_w1.wait_recv()
        for node in range(2):
            for block in range(2):
                digit = (x_hi + block) % 2
                columns = slice(block * LANES, block * LANES + LANES)
                high, low = halves(b_v[1, node, y_hi, digit])
                l1[node, 0:128, columns] = high
                l1[node, 256:384, columns] = low
                high, low = halves(w1[node, digit])
                l1[node, 128:256, columns] = high
                l1[node, 384:512, columns] = low

    def prepare_2():
        load_b(2).wait()
        for node in range(2):
            for block in range(4):
                high, low = halves(
                    b_v[2, node, (z_lo + block // 2) % 2, (core + block) % 2]
                )
                columns = slice(block * LANES, block * LANES + LANES)
                l2[node, 0:128, columns] = high
                l2[node, 128:256, columns] = low

    def prepare_3():
        load_b(3).wait()
        send_w3.wait_recv()
        for node in range(2):
            for block in range(2):
                digit = (y_lo + block) % 2
                columns = slice(block * LANES, block * LANES + LANES)
                high, low = halves(b_v[3, node, digit, z_hi])
                l3[node, 0:128, columns] = high
                l3[node, 256:384, columns] = low
                high, low = halves(w3[node, digit])
                l3[node, 128:256, columns] = high
                l3[node, 384:512, columns] = low

    def prepare_e():
        load_e.wait()
        for node in range(2):
            high, low = halves(e_v[node])
            e_w[node, :, 0:LANES] = high
            e_w[node, :, LANES : 2 * LANES] = low

    def level_0(panel):
        first = 2 * panel
        exchange(X1, first).wait_recv()
        exchange(X1, first + 1).wait_recv()
        value = jnp.concatenate([xb[first], xb[first + 1], xr[first], xr[first + 1]], 0)
        both = product(l0[...], value)
        yb[first] = both[:LANES]
        yb[first + 1] = both[LANES:]
        exchange(X2, first).start()
        exchange(X2, first + 1).start()

    def level_1(sub):
        exchange(X2, sub).wait_recv()
        both = product(l1[sub % 2], jnp.concatenate([yb[sub], yr[sub]], 0))
        zs[sub] = both[LANES:]
        exchange(Y2, sub).start()
        zo[sub] = both[:LANES]

    def sum_1(sub):
        exchange(Y2, sub).wait_recv()
        cb[sub] = zo[sub] + zr[sub]
        exchange(Z1, sub).start()
        exchange(CO, sub).start()

    def forward(sub):
        exchange(Z1, sub).wait_recv()
        exchange(FW, sub).start()

    def level_2(sub):
        exchange(CO, sub).wait_recv()
        exchange(FW, sub).wait_recv()
        value = jnp.concatenate([cb[sub], cor[sub], czr[sub], cfr[sub]], 0)
        db[sub] = product(l2[sub % 2], value)
        exchange(Y1, sub).start()

    def level_3(sub):
        exchange(Y1, sub).wait_recv()
        both = product(l3[sub % 2], jnp.concatenate([db[sub], dr[sub]], 0))
        fs[sub] = both[LANES:]
        exchange(Z2, sub).start()
        fo[sub] = both[:LANES]

    def sum_3(sub):
        exchange(Z2, sub).wait_recv()
        high, low = halves(fo[sub] + fr[sub])
        pair = jnp.concatenate([high, low], 1)
        both = dot(e_w[sub % 2], jnp.concatenate([pair, pair], 0))
        columns = pl.ds(pl.multiple_of(sub // 2 * LANES, LANES), LANES)
        out[sub % 2, :, columns] = out[sub % 2, :, columns] + both[:, :LANES] + both[:, LANES:]

    def near_tile(tile):
        load_n(tile).wait()
        node, row = tile // 4, pl.multiple_of(tile % 4 * 256, 256)
        high, low = halves(n_v[tile])
        right = s_hi[node]
        out[node, pl.ds(row, 256), :] = (
            dot(high, right) + dot(low, right) + dot(high, s_lo[node])
        )

    def when_sub(step, start, body):
        sub = step - start

        @pl.when((sub >= 0) & (sub < SUBS))
        def _():
            body(sub)

    def iteration(step, _):
        when_sub(step, AT_SUM3, sum_3)
        when_sub(step, AT_L3, level_3)
        when_sub(step, AT_L2, level_2)
        when_sub(step, AT_FWD, forward)
        when_sub(step, AT_SUM1, sum_1)
        when_sub(step, AT_L1, level_1)

        odd = step - AT_L0 - 1

        @pl.when((odd >= 0) & (odd < SUBS) & (odd % 2 == 0))
        def _():
            level_0(odd // 2)

        sub = step - AT_SEND

        @pl.when((sub >= 2) & (sub < SUBS))
        def _():
            exchange(X1, sub).start()

        tile = step - NEAR_AT

        @pl.when((tile >= 0) & (tile < TILES - 2))
        def _():
            load_n(tile + 2).start()

        @pl.when(tile == TILES - 2)
        def _():
            load_e.start()

        when_sub(step, NEAR_AT, near_tile)
        pl.when(step == 1)(prepare_1)
        pl.when(step == 4)(prepare_2)
        pl.when(step == 6)(prepare_3)
        pl.when(step == NEAR_AT + TILES)(prepare_e)
        return 0

    lax.fori_loop(0, AT_SUM3 + SUBS, iteration, 0)

    def drain(sub, _):
        for step in range(8):
            exchange(step, sub).wait_send()
        return 0

    lax.fori_loop(0, SUBS, drain, 0)
    send_w1.wait_send()
    send_w3.wait_send()


def body(sources, near_field, project_factor, expand_factor, butterfly):
    nodes, leaf, _ = near_field.shape
    rhs = sources.shape[1]
    rank = project_factor.shape[1]
    f32, bf16 = jnp.float32, jnp.bfloat16
    block = pltpu.VMEM((SUBS, rank, LANES), f32)
    dma = pltpu.SemaphoreType.DMA
    result = pl.pallas_call(
        kernel,
        out_shape=pltpu.VMEM((nodes, leaf, rhs), f32),
        in_specs=[pl.BlockSpec(memory_space=pl.ANY)] * 5,
        out_specs=pl.BlockSpec(memory_space=pltpu.VMEM),
        scratch_shapes=[
            pltpu.VMEM((4, nodes, leaf, LANES), f32),
            pltpu.VMEM((TILES, 256, leaf), f32),
            pltpu.VMEM((nodes, leaf, rank), f32),
            pltpu.VMEM((nodes, leaf, rank), f32),
            pltpu.VMEM((4, nodes, 2, 2, rank, rank), f32),
            pltpu.VMEM((nodes, leaf, rhs), bf16),
            pltpu.VMEM((nodes, leaf, rhs), bf16),
            pltpu.VMEM((nodes, 2 * rank, leaf), bf16),
            pltpu.VMEM((nodes, leaf, 2 * rank), bf16),
            pltpu.VMEM((4 * rank, 4 * rank), bf16),
            pltpu.VMEM((nodes, 4 * rank, 2 * rank), bf16),
            pltpu.VMEM((nodes, 2 * rank, 4 * rank), bf16),
            pltpu.VMEM((nodes, 4 * rank, 2 * rank), bf16),
            pltpu.VMEM((nodes, 2, rank, rank), f32),
            pltpu.VMEM((nodes, 2, rank, rank), f32),
        ]
        + [block] * 16
        + [
            dma((4,)), dma((TILES,)), dma((2,)), dma((1,)), dma((4,)),
            dma((2,)), dma((2,)), dma((8, SUBS)), dma((8, SUBS)),
        ],
        compiler_params=pltpu.CompilerParams(
            collective_id=0, has_side_effects=True, vmem_limit_bytes=50 * 1024 * 1024
        ),
        name="butterfly",
    )(
        sources.reshape(nodes, leaf, rhs),
        near_field.reshape(TILES, 256, leaf),
        project_factor.reshape(nodes, leaf, rank),
        expand_factor.reshape(nodes, leaf, rank),
        butterfly.reshape(butterfly.shape[0], nodes, 2, 2, rank, rank),
    )
    return result.reshape(nodes * leaf, rhs)


def solution(mesh):
    in_specs = (
        P(("outer", "inner"), None),
        P(("outer", "inner"), None, None),
        P(("outer", "inner"), None),
        P(("outer", "inner"), None),
        P(None, ("outer", "inner"), None, None, None),
    )
    out_specs = P(("outer", "inner"), None)
    return jax.shard_map(body, mesh=mesh, in_specs=in_specs, out_specs=out_specs, check_vma=False)
```

time: 126 us -> 65.2 us (0.52)
  Pallas kernels: 0 us -> 63 us
  waiting for transfers between devices: 43.7 us -> 0 us
  matrix products: 38.3 us -> 0 us
  starting transfers between devices: 23 us -> 0 us
  other arithmetic: 16.1 us -> 0 us
  local copies, waits for them, and re-layouts: 3.6 us -> 2.02 us
    pallas_call x0 -> x1, Pallas kernels: none -> 63 us  [body(): pl.pallas_call(kernel, out_shape=pltpu.VMEM((nodes, leaf, rhs), f32), in_...]
    ppermute x14 -> x0, waiting for transfers between devices: 43.7 us -> none  [from_partner(): return lax.ppermute(value, axis, pairs)]
    dot_general x14 -> x0, matrix products: 38.3 us -> none  [the longest x2 20 us: run_block(): jnp.einsum('cmn,cnr->cmr', near_field, source_rows, precision=HIGHEST)]
    ppermute x14 -> x0, starting transfers between devices: 23 us -> none  [from_partner(): return lax.ppermute(value, axis, pairs)]
    select_n x14 -> x0, other arithmetic: 13.4 us -> none  [swap_section(): jnp.where(my_bit == 0, jnp.concatenate([gathered_set, partner], 0), jnp.c...]
    slice x1 -> x0, local copies, waits for them, and re-layouts: 2.64 us -> none  [body(): sources[:, :middle]]
    concatenate x1 -> x0, other arithmetic: 2.55 us -> none  [body(): return jnp.concatenate([first_half, second_half], 1)]
  transfers between devices with their start and end apart: 14 -> 0, of which waited for: 8 -> 0; matrix products, arithmetic and copies ran while one was open for 35% -> 0% of each run, Pallas kernels for 0% -> 0%
where the time goes in v1:
time: 65.2 us; the launch traced here: 65.1 us
  Pallas kernels  63 us (97%)
  local copies, waits for them, and re-layouts  2.02 us (3%)
    pallas_call x1, Pallas kernels, body(): pl.pallas_call(kernel, out_shape=pltpu.VMEM((nodes, leaf, rhs), f32), in_...  63 us
    unnamed x1, local copies, waits for them, and re-layouts  2.02 us

profile of v1, /device:TPU:0, one launch (start us, length us, event | category | flops | bytes accessed | tf_op | source)
XLA Modules:
  0.0 65.1 jit_solution(1795159716759157403)
XLA Ops:
  0.0 63.0 %butterfly.1 = f32[2,1024,512]{2,1,0:T(8,128)S(1)} custom-call(f32[2,1024,512]{2,1,0:T(8,128)} %bitcast.8, f32[8,256,1024]{2,1,0:T(8,128)} %bitcast.7, f32[2,1024,128]{2,1,0:T(8,128)} %bitcast.10, f32[2,1024,128]{2,1,0:T(8,128)} %bitcast.11, f32[4,2,2,2,128,128]{5,4,3,2,1,0:T(8,128)} %bitcast.9), custom_call_target="tpu_custom_call" | custom-call | tf_op jit(solution)/shard_map/butterfly/pallas_call | solution.py:332
  63.1 2.0 %copy.7 = f32[2048,512]{1,0:T(8,128)} copy(f32[2048,512]{1,0:T(8,128)S(1)} %bitcast.6) | data formatting | bytes 8388608

commit v2 on v1

--- a/solution.py
+++ b/solution.py
@@ -12,8 +12,9 @@
 SUBS = 8
 TILES = 8
 X1, X2, Y2, Z1, CO, FW, Y1, Z2 = range(8)
-AT_SEND, AT_L0, AT_L1, AT_SUM1, AT_FWD, AT_L2, AT_L3, AT_SUM3 = 0, 2, 4, 6, 8, 9, 11, 13
+AT_SEND, AT_L0, AT_L1, AT_SUM1, AT_FWD, AT_L2, AT_L3, AT_SUM3 = 0, 3, 7, 10, 13, 15, 18, 22
 NEAR_AT = 0
+AHEAD = 6
 
 
 def halves(value):
@@ -102,48 +103,59 @@
         load_s(panel).start()
     load_b(0).start()
 
+    pl.semaphore_wait(barrier, 7)
+
+    def exchange_w1(node):
+        return pltpu.make_async_remote_copy(
+            src_ref=fly.at[1, node, 1 - y_hi],
+            dst_ref=w1.at[node],
+            send_sem=w_send.at[node],
+            recv_sem=w_recv.at[node],
+            device_id=where[Y2],
+            device_id_type=MESH,
+        )
+
+    def exchange_w3(node):
+        return pltpu.make_async_remote_copy(
+            src_ref=fly.at[3, node, :, 1 - z_hi],
+            dst_ref=w3.at[node],
+            send_sem=w_send.at[2 + node],
+            recv_sem=w_recv.at[2 + node],
+            device_id=where[Z2],
+            device_id_type=MESH,
+        )
+
     for node in range(2):
-        load_p(node).wait()
-        high, low = halves(p_v[node].T)
-        p_t[node, 0:LANES, :] = high
-        p_t[node, LANES : 2 * LANES, :] = low
-
-    pl.semaphore_wait(barrier, 7)
-    send_w1 = pltpu.make_async_remote_copy(
-        src_ref=fly.at[1, :, 1 - y_hi],
-        dst_ref=w1,
-        send_sem=w_send.at[0],
-        recv_sem=w_recv.at[0],
-        device_id=where[Y2],
-        device_id_type=MESH,
-    )
-    send_w3 = pltpu.make_async_remote_copy(
-        src_ref=fly.at[3, :, :, 1 - z_hi],
-        dst_ref=w3,
-        send_sem=w_send.at[1],
-        recv_sem=w_recv.at[1],
-        device_id=where[Z2],
-        device_id_type=MESH,
-    )
-    send_w1.start()
-    send_w3.start()
-
-    def project(panel, _):
-        load_s(panel).wait()
-        for node in range(2):
-            high, low = halves(s_v[panel, node])
-            columns = pl.ds(pl.multiple_of(panel * LANES, LANES), LANES)
-            s_hi[node, :, columns] = high
-            s_lo[node, :, columns] = low
-            both = dot(p_t[node], jnp.concatenate([high, low], 1))
-            xb[2 * panel + node] = (
-                both[:LANES, :LANES] + both[:LANES, LANES:] + both[LANES:, :LANES]
-            )
+        exchange_w1(node).start()
+        exchange_w3(node).start()
+
+    def project(sub, _):
+        panel, node = sub // 2, sub % 2
 
         @pl.when(panel == 0)
         def _():
-            exchange(X1, 0).start()
-            exchange(X1, 1).start()
+            load_p(node).wait()
+            high, low = halves(p_v[node].T)
+            p_t[node, 0:LANES, :] = high
+            p_t[node, LANES : 2 * LANES, :] = low
+
+        @pl.when(node == 0)
+        def _():
+            load_s(panel).wait()
+
+        high, low = halves(s_v[panel, node])
+        columns = pl.ds(pl.multiple_of(panel * LANES, LANES), LANES)
+        s_hi[node, :, columns] = high
+        s_lo[node, :, columns] = low
+        both = dot(p_t[node], jnp.concatenate([high, low], 1))
+        xb[sub] = both[:LANES, :LANES] + both[:LANES, LANES:] + both[LANES:, :LANES]
+
+        @pl.when(sub < AHEAD)
+        def _():
+            exchange(X1, sub).start()
+
+        @pl.when(sub == 1)
+        def _():
             for level in range(1, 4):
                 load_b(level).start()
             load_n(0).start()
@@ -151,7 +163,7 @@
 
         return 0
 
-    lax.fori_loop(0, 4, project, 0)
+    lax.fori_loop(0, SUBS, project, 0)
 
     load_b(0).wait()
     for node in range(2):
@@ -163,7 +175,6 @@
 
     def prepare_1():
         load_b(1).wait()
-        send_w1.wait_recv()
         for node in range(2):
             for block in range(2):
                 digit = (x_hi + block) % 2
@@ -171,6 +182,13 @@
                 high, low = halves(b_v[1, node, y_hi, digit])
                 l1[node, 0:128, columns] = high
                 l1[node, 256:384, columns] = low
+
+    def receive_1():
+        for node in range(2):
+            exchange_w1(node).wait_recv()
+            for block in range(2):
+                digit = (x_hi + block) % 2
+                columns = slice(block * LANES, block * LANES + LANES)
                 high, low = halves(w1[node, digit])
                 l1[node, 128:256, columns] = high
                 l1[node, 384:512, columns] = low
@@ -188,8 +206,8 @@
 
     def prepare_3():
         load_b(3).wait()
-        send_w3.wait_recv()
         for node in range(2):
+            exchange_w3(node).wait_recv()
             for block in range(2):
                 digit = (y_lo + block) % 2
                 columns = slice(block * LANES, block * LANES + LANES)
@@ -257,13 +275,19 @@
         columns = pl.ds(pl.multiple_of(sub // 2 * LANES, LANES), LANES)
         out[sub % 2, :, columns] = out[sub % 2, :, columns] + both[:, :LANES] + both[:, LANES:]
 
-    def near_tile(tile):
-        load_n(tile).wait()
+    def near_tile(part):
+        tile = part // 2
+
+        @pl.when(part % 2 == 0)
+        def _():
+            load_n(tile).wait()
+
         node, row = tile // 4, pl.multiple_of(tile % 4 * 256, 256)
+        columns = pl.ds(pl.multiple_of(part % 2 * 256, 256), 256)
         high, low = halves(n_v[tile])
-        right = s_hi[node]
-        out[node, pl.ds(row, 256), :] = (
-            dot(high, right) + dot(low, right) + dot(high, s_lo[node])
+        right = s_hi[node, :, columns]
+        out[node, pl.ds(row, 256), columns] = (
+            dot(high, right) + dot(low, right) + dot(high, s_lo[node, :, columns])
         )
 
     def when_sub(step, start, body):
@@ -279,6 +303,7 @@
         when_sub(step, AT_L2, level_2)
         when_sub(step, AT_FWD, forward)
         when_sub(step, AT_SUM1, sum_1)
+        pl.when(step == AT_L1)(receive_1)
         when_sub(step, AT_L1, level_1)
 
         odd = step - AT_L0 - 1
@@ -289,25 +314,28 @@
 
         sub = step - AT_SEND
 
-        @pl.when((sub >= 2) & (sub < SUBS))
+        @pl.when((sub >= AHEAD) & (sub < SUBS))
         def _():
             exchange(X1, sub).start()
 
-        tile = step - NEAR_AT
-
-        @pl.when((tile >= 0) & (tile < TILES - 2))
-        def _():
-            load_n(tile + 2).start()
-
-        @pl.when(tile == TILES - 2)
+        part = step - NEAR_AT
+
+        @pl.when((part >= 0) & (part < TILES - 2))
+        def _():
+            load_n(part + 2).start()
+
+        @pl.when(part == TILES - 2)
         def _():
             load_e.start()
 
-        when_sub(step, NEAR_AT, near_tile)
-        pl.when(step == 1)(prepare_1)
-        pl.when(step == 4)(prepare_2)
-        pl.when(step == 6)(prepare_3)
-        pl.when(step == NEAR_AT + TILES)(prepare_e)
+        @pl.when((part >= 0) & (part < 2 * TILES))
+        def _():
+            near_tile(part)
+
+        pl.when(step == 0)(prepare_1)
+        pl.when(step == 5)(prepare_2)
+        pl.when(step == 7)(prepare_3)
+        pl.when(step == AT_SUM3 - 1)(prepare_e)
         return 0
 
     lax.fori_loop(0, AT_SUM3 + SUBS, iteration, 0)
@@ -318,8 +346,9 @@
         return 0
 
     lax.fori_loop(0, SUBS, drain, 0)
-    send_w1.wait_send()
-    send_w3.wait_send()
+    for node in range(2):
+        exchange_w1(node).wait_send()
+        exchange_w3(node).wait_send()
 
 
 def body(sources, near_field, project_factor, expand_factor, butterfly):
@@ -354,7 +383,7 @@
         + [block] * 16
         + [
             dma((4,)), dma((TILES,)), dma((2,)), dma((1,)), dma((4,)),
-            dma((2,)), dma((2,)), dma((8, SUBS)), dma((8, SUBS)),
+            dma((4,)), dma((4,)), dma((8, SUBS)), dma((8, SUBS)),
         ],
         compiler_params=pltpu.CompilerParams(
             collective_id=0, has_side_effects=True, vmem_limit_bytes=50 * 1024 * 1024

time: 65.2 us -> 56.7 us (0.87)
  Pallas kernels: 63 us -> 54.5 us
    pallas_call x1, Pallas kernels: 63 us -> 54.5 us  [body(): pl.pallas_call(kernel, out_shape=pltpu.VMEM((nodes, leaf, rhs), f32), in_...]
where the time goes in v2:
time: 56.7 us; the launch traced here: 56.6 us
  Pallas kernels  54.5 us (96%)
  local copies, waits for them, and re-layouts  2.02 us (4%)
    pallas_call x1, Pallas kernels, body(): pl.pallas_call(kernel, out_shape=pltpu.VMEM((nodes, leaf, rhs), f32), in_...  54.5 us
    unnamed x1, local copies, waits for them, and re-layouts  2.02 us

profile of v2, /device:TPU:0, one launch (start us, length us, event | category | flops | bytes accessed | tf_op | source)
XLA Modules:
  0.0 56.6 jit_solution(15916756517234010324)
XLA Ops:
  0.0 54.5 %butterfly.1 = f32[2,1024,512]{2,1,0:T(8,128)S(1)} custom-call(f32[2,1024,512]{2,1,0:T(8,128)} %bitcast.8, f32[8,256,1024]{2,1,0:T(8,128)} %bitcast.7, f32[2,1024,128]{2,1,0:T(8,128)} %bitcast.10, f32[2,1024,128]{2,1,0:T(8,128)} %bitcast.11, f32[4,2,2,2,128,128]{5,4,3,2,1,0:T(8,128)} %bitcast.9), custom_call_target="tpu_custom_call" | custom-call | tf_op jit(solution)/shard_map/butterfly/pallas_call | solution.py:361
  54.6 2.0 %copy.7 = f32[2048,512]{1,0:T(8,128)} copy(f32[2048,512]{1,0:T(8,128)S(1)} %bitcast.6) | data formatting | bytes 8388608

commit v3 on v2

--- a/solution.py
+++ b/solution.py
@@ -12,9 +12,8 @@
 SUBS = 8
 TILES = 8
 X1, X2, Y2, Z1, CO, FW, Y1, Z2 = range(8)
-AT_SEND, AT_L0, AT_L1, AT_SUM1, AT_FWD, AT_L2, AT_L3, AT_SUM3 = 0, 3, 7, 10, 13, 15, 18, 22
+AT_SEND, AT_L0, AT_L1, AT_SUM1, AT_FWD, AT_L2, AT_L3, AT_SUM3 = 0, 3, 8, 11, 14, 16, 19, 23
 NEAR_AT = 0
-AHEAD = 6
 
 
 def halves(value):
@@ -44,6 +43,7 @@
     inner = lax.axis_index("inner")
     x_lo, x_hi, y_hi = inner % 2, inner // 2 % 2, inner // 4
     core, z_lo, z_hi, y_lo = outer % 2, outer // 2 % 2, outer // 4 % 2, outer // 8
+    ahead = 8 - 4 * core
     inner_x1 = inner + 1 - 2 * x_lo
     inner_x2 = inner + 2 - 4 * x_hi
     inner_y2 = inner + 4 - 8 * y_hi
@@ -150,7 +150,7 @@
         both = dot(p_t[node], jnp.concatenate([high, low], 1))
         xb[sub] = both[:LANES, :LANES] + both[:LANES, LANES:] + both[LANES:, :LANES]
 
-        @pl.when(sub < AHEAD)
+        @pl.when(sub < ahead)
         def _():
             exchange(X1, sub).start()
 
@@ -298,7 +298,6 @@
             body(sub)
 
     def iteration(step, _):
-        when_sub(step, AT_SUM3, sum_3)
         when_sub(step, AT_L3, level_3)
         when_sub(step, AT_L2, level_2)
         when_sub(step, AT_FWD, forward)
@@ -311,10 +310,11 @@
         @pl.when((odd >= 0) & (odd < SUBS) & (odd % 2 == 0))
         def _():
             level_0(odd // 2)
+        when_sub(step, AT_SUM3, sum_3)
 
         sub = step - AT_SEND
 
-        @pl.when((sub >= AHEAD) & (sub < SUBS))
+        @pl.when((sub >= ahead) & (sub < SUBS))
         def _():
             exchange(X1, sub).start()
 

time: 56.7 us -> 56.1 us (0.989)
    pallas_call x1, Pallas kernels: 54.5 us -> 54 us  [body(): pl.pallas_call(kernel, out_shape=pltpu.VMEM((nodes, leaf, rhs), f32), in_...]
where the time goes in v3:
time: 56.1 us; the launch traced here: 56 us
  Pallas kernels  54 us (96%)
  local copies, waits for them, and re-layouts  2.02 us (4%)
    pallas_call x1, Pallas kernels, body(): pl.pallas_call(kernel, out_shape=pltpu.VMEM((nodes, leaf, rhs), f32), in_...  54 us
    unnamed x1, local copies, waits for them, and re-layouts  2.02 us

profile of v3, /device:TPU:0, one launch (start us, length us, event | category | flops | bytes accessed | tf_op | source)
XLA Modules:
  0.0 56.0 jit_solution(16819945233689536481)
XLA Ops:
  0.0 54.0 %butterfly.1 = f32[2,1024,512]{2,1,0:T(8,128)S(1)} custom-call(f32[2,1024,512]{2,1,0:T(8,128)} %bitcast.8, f32[8,256,1024]{2,1,0:T(8,128)} %bitcast.7, f32[2,1024,128]{2,1,0:T(8,128)} %bitcast.10, f32[2,1024,128]{2,1,0:T(8,128)} %bitcast.11, f32[4,2,2,2,128,128]{5,4,3,2,1,0:T(8,128)} %bitcast.9), custom_call_target="tpu_custom_call" | custom-call | tf_op jit(solution)/shard_map/butterfly/pallas_call | solution.py:361
  54.0 2.0 %copy.7 = f32[2048,512]{1,0:T(8,128)} copy(f32[2048,512]{1,0:T(8,128)S(1)} %bitcast.6) | data formatting | bytes 8388608

commit v4 on v3

--- a/solution.py
+++ b/solution.py
@@ -12,7 +12,7 @@
 SUBS = 8
 TILES = 8
 X1, X2, Y2, Z1, CO, FW, Y1, Z2 = range(8)
-AT_SEND, AT_L0, AT_L1, AT_SUM1, AT_FWD, AT_L2, AT_L3, AT_SUM3 = 0, 3, 8, 11, 14, 16, 19, 23
+AT_SEND, AT_L0, AT_L1, AT_SUM1, AT_FWD, AT_L2, AT_L3, AT_SUM3 = 0, 2, 7, 10, 13, 15, 18, 22
 NEAR_AT = 0
 
 

time: 56.1 us -> 58.5 us (1.043)
  Pallas kernels: 54 us -> 56 us
    pallas_call x1, Pallas kernels: 54 us -> 56 us  [body(): pl.pallas_call(kernel, out_shape=pltpu.VMEM((nodes, leaf, rhs), f32), in_...]
where the time goes in v4:
time: 58.5 us; the launch traced here: 58 us
  Pallas kernels  56 us (96%)
  local copies, waits for them, and re-layouts  2.02 us (3%)
    pallas_call x1, Pallas kernels, body(): pl.pallas_call(kernel, out_shape=pltpu.VMEM((nodes, leaf, rhs), f32), in_...  56 us
    unnamed x1, local copies, waits for them, and re-layouts  2.02 us

profile of v4, /device:TPU:0, one launch (start us, length us, event | category | flops | bytes accessed | tf_op | source)
XLA Modules:
  0.0 58.0 jit_solution(13933223601103432455)
XLA Ops:
  0.0 56.0 %butterfly.1 = f32[2,1024,512]{2,1,0:T(8,128)S(1)} custom-call(f32[2,1024,512]{2,1,0:T(8,128)} %bitcast.8, f32[8,256,1024]{2,1,0:T(8,128)} %bitcast.7, f32[2,1024,128]{2,1,0:T(8,128)} %bitcast.10, f32[2,1024,128]{2,1,0:T(8,128)} %bitcast.11, f32[4,2,2,2,128,128]{5,4,3,2,1,0:T(8,128)} %bitcast.9), custom_call_target="tpu_custom_call" | custom-call | tf_op jit(solution)/shard_map/butterfly/pallas_call | solution.py:361
  56.0 2.0 %copy.7 = f32[2048,512]{1,0:T(8,128)} copy(f32[2048,512]{1,0:T(8,128)S(1)} %bitcast.6) | data formatting | bytes 8388608
